TPU v7x, 512 devices: a 8x2x16 block of a 8x16x16 slice. The times are simulated.
512 devices in a mesh: groups: 2 (over y), seq: 16 (over z), head: 8 (over x), layer: 2 (over core).
Axes of the slice: x: 8, y: 2, z: 16, core: 2. Of those that a mesh axis runs over, the one named last changes fastest.
The devices are a block of a 8x16x16 slice.
Arguments:
- kv_cache: bfloat16 [2, 2, 8, 16384, 8, 128], P(None, 'layer', 'groups', 'seq', 'head'), parts along dimension 2, may hold values from -800 to 800
- valid_blocks: int32 [8], P('groups'), parts along dimension 0, may hold values from 1 to 128, 256 in all
Outputs:
- decode_cache: bfloat16 [2, 2, 32, 4096, 8, 128], P(None, 'layer', ('groups', 'seq'), None, 'head'), parts along dimension 2
- centers: float32 [2, 2, 8, 8, 128], P(None, 'layer', 'groups', 'head'), parts along dimension 2
- scales: float32 [2, 2, 8, 8, 128], P(None, 'layer', 'groups', 'head'), parts along dimension 2
There are 2 independent parts, one for each index of `groups`. A program takes and returns all parts, laid end to end along the dimension named above; each array names one. Nothing has to cross between parts.
Inputs may be any that keep to these rules, and one draw needn't show every extreme that they name: `valid_blocks`: the counts of the 4 users sum to 256, and the largest equals 128.
All inputs are finite; a program needn't handle non-finite values.
Results may differ from a plain program's by a relative error of at most 0.001.
Values may be sent and summed in bfloat16 or wider, within the bound.
No kernel may reach another device: no remote copies, remote signals or barrier semaphores. Data moves between devices by JAX's collectives and lax.ppermute only.
A program may use at most 64 MiB of HBM per device.

v0:
```python
import jax
import jax.numpy as jnp
from jax import lax
from jax.sharding import PartitionSpec as P

BLOCK = 128


epsilon = 1e-06
ceiling_value = 3e38


def from_everyone(array, axis):
    copies = jnp.broadcast_to(array, (lax.axis_size(axis), *array.shape))
    return lax.all_to_all(copies, axis, split_axis=0, concat_axis=0, tiled=True)


def all_in_one(array, axis):
    leaves = jax.tree.leaves(array)
    turns = sorted(range(len(leaves)), key=lambda k: -leaves[k].size)
    width = (1, *leaves[turns[0]].shape)[-1]
    lines = [
        jnp.pad(leaves[k].reshape(-1), (0, -leaves[k].size % width)).reshape(-1, width)
        for k in turns
    ]
    both, at, found = (from_everyone(jnp.concatenate(lines), axis), 0, {})
    for k, line in zip(turns, lines):
        share = both[:, at : at + len(line)].reshape(len(both), -1)
        found[k] = share[:, : leaves[k].size].reshape(-1, *leaves[k].shape)
        at += len(line)
    numbers = iter(range(len(leaves)))
    return jax.tree.map(lambda _: found[next(numbers)], array)


def combined_pairwise(pieces, combine):
    while len(jax.tree.leaves(pieces)[0]) > 1:
        pieces = jax.vmap(combine)(
            *(jax.tree.map(lambda part: part[side::2], pieces) for side in (0, 1))
        )
    return jax.tree.map(lambda part: part[0], pieces)


def joined_all(array, axis, combine):
    pieces = all_in_one(array, axis)
    return combined_pairwise(pieces, combine)


def combine_stats(left_side, right_side):
    return (
        left_side[0] + right_side[0],
        jnp.maximum(left_side[1], right_side[1]),
        jnp.minimum(left_side[2], right_side[2]),
    )


def on_device(kv_cache, valid_blocks):
    kind_count, layer_dev, user_count, per_dev, heads_dev, head_dim = kv_cache.shape
    owners = lax.axis_size("seq")
    quarter = owners // user_count
    part_len = per_dev // quarter
    seq_index = lax.axis_index("seq")
    lengths = valid_blocks * BLOCK
    values = kv_cache.astype(jnp.float32)
    position = seq_index * per_dev + jnp.arange(per_dev, dtype=jnp.int32)
    is_live = position[None, :] < lengths[:, None]
    live_mask = is_live[None, None, :, :, None, None]
    local_sum = jnp.sum(jnp.where(live_mask, values, 0.0), axis=3)
    user_lengths = lengths.astype(jnp.float32)[None, None, :, None, None]
    local_high = jnp.max(jnp.where(live_mask, values, -ceiling_value), axis=3)
    local_low = jnp.min(jnp.where(live_mask, values, ceiling_value), axis=3)
    totals, highest, lowest = joined_all((local_sum, local_high, local_low), "seq", combine_stats)
    centers = totals / user_lengths
    spread = jnp.maximum(highest - centers, centers - lowest)
    scales = spread + epsilon
    normed = jnp.where(
        live_mask, (values - centers[:, :, :, None]) / scales[:, :, :, None], 0.0
    ).astype(jnp.bfloat16)
    outgoing = normed.reshape(
        kind_count, layer_dev, user_count * quarter, part_len, heads_dev, head_dim
    )
    received = lax.all_to_all(outgoing, "seq", split_axis=2, concat_axis=2, tiled=True)
    arranged = received.reshape(kind_count, layer_dev, 1, owners * part_len, heads_dev, head_dim)
    return (arranged, centers, scales)


def solution(mesh):
    in_specs = (P(None, "layer", "groups", "seq", "head", None), P("groups"))
    out_specs = (
        P(None, "layer", ("groups", "seq"), None, "head", None),
        P(None, "layer", "groups", "head", None),
        P(None, "layer", "groups", "head", None),
    )
    return jax.shard_map(
        on_device, mesh=mesh, in_specs=in_specs, out_specs=out_specs, check_vma=False
    )
```

profile of v0, /device:TPU:78, one launch (start us, length us, event | category | flops | bytes accessed | tf_op | source)
XLA Modules:
  0.0 169.0 jit_solution(14551029651689146613)
XLA Ops:
  0.6 0.0 copy-start
  0.6 0.8 fusion.8
  1.5 0.1 broadcast_compare_fusion
  1.5 3.1 %fusion = (f32[2,4,128]{2,1,0:T(4,128)S(1)}, f32[2,4,128]{2,1,0:T(4,128)S(1)}, f32[2,4,128]{2,1,0:T(4,128)S(1)}) fusion(bf16[2,1,4,1024,1,128]{5,3,4,2,1,0:T(8,128)(2,1)} %param.2, pred[4,1024]{1,0:T(4,128)(4,1)S(1)} %broadcast_compare_fusion), kind=kLoop, calls=%fused_computation.4 | loop fusion | flops 7336960 | bytes 2113536 | tf_op jit(solution)/shard_map/reduce_sum | solution.py:67
  4.7 59.7 %all_to_all.10 = f32[16,24,128]{2,1,0:T(8,128)S(1)} all-to-all(f32[16,24,128]{2,1,0:T(8,128)S(1)} %broadcast_in_dim.41), channel_id=1, replica_groups=mesh['groups'=2,'seq'=16,'head'=8,'layer'=2] {'seq'}, dimensions={0} | all-to-all | bytes 393216 | tf_op jit(solution)/shard_map/all_to_all | solution.py:15
  64.5 0.1 fusion.7
  64.6 0.0 copy-done
  64.6 1.0 fusion.5
  65.6 1.5 copy.12
  67.1 5.2 %all-to-all-start.1 = ((bf16[2,1,16,256,1,128]{5,3,0,4,1,2:T(8,128)(2,1)}), bf16[2,1,16,256,1,128]{5,3,0,4,1,2:T(8,128)(2,1)S(1)}, u32[]{:S(2)}, u32[]{:S(2)}) async-start(bf16[2,1,16,256,1,128]{5,3,0,4,1,2:T(8,128)(2,1)} %copy.12), calls=%async_computation.1 | async-start | bytes 4194304 | tf_op jit(solution)/shard_map/all_to_all | solution.py:81
  72.3 0.1 bitcast_subtract_fusion
  72.4 0.0 copy-start.1
  72.4 0.6 maximum_add_fusion
  73.0 94.5 %all-to-all-done.1 = bf16[2,1,16,256,1,128]{5,3,0,4,1,2:T(8,128)(2,1)S(1)} async-done(((bf16[2,1,16,256,1,128]{5,3,0,4,1,2:T(8,128)(2,1)}), bf16[2,1,16,256,1,128]{5,3,0,4,1,2:T(8,128)(2,1)S(1)}, u32[]{:S(2)}, u32[]{:S(2)}) %all-to-all-start.1) | async-done | bytes 2097184 | tf_op jit(solution)/shard_map/all_to_all | solution.py:81
  167.5 1.5 copy.13
  169.0 0.0 copy-done.1
  (12 shorter events, 0.1 us)
Async XLA Ops:
  0.6 63.9 %copy-start = (bf16[2,1,4,1024,1,128]{5,3,4,2,1,0:T(8,128)(2,1)S(1)}, bf16[2,1,4,1024,1,128]{5,3,4,2,1,0:T(8,128)(2,1)}, u32[]{:S(2)}) copy-start(bf16[2,1,4,1024,1,128]{5,3,4,2,1,0:T(8,128)(2,1)} %param.2) | copy-start | bytes 6291460
  67.1 100.4 %all-to-all-start.1 = ((bf16[2,1,16,256,1,128]{5,3,0,4,1,2:T(8,128)(2,1)}), bf16[2,1,16,256,1,128]{5,3,0,4,1,2:T(8,128)(2,1)S(1)}, u32[]{:S(2)}, u32[]{:S(2)}) async-start(bf16[2,1,16,256,1,128]{5,3,0,4,1,2:T(8,128)(2,1)} %copy.12), calls=%async_computation.1 | async-start | bytes 4194304 | tf_op jit(solution)/shard_map/all_to_all | solution.py:81
  72.4 96.7 %copy-start.1 = (f32[2,1,4,1,128]{4,2,0,3,1:T(4,128)}, f32[2,1,4,1,128]{4,2,0,3,1:T(4,128)S(1)}, u32[]{:S(2)}) copy-start(f32[2,1,4,1,128]{4,2,0,3,1:T(4,128)S(1)} %get-tuple-element.16) | copy-start | bytes 12292
where the time goes:
time: 169 us
  waiting for transfers between devices  94.5 us (56%)
  blocking collectives  59.7 us (35%)
  other arithmetic  5.83 us (3%)
  starting transfers between devices  5.24 us (3%)
  local copies, waits for them, and re-layouts  3.05 us (2%)
    all_to_all x1, waiting for transfers between devices, on_device(): lax.all_to_all(outgoing, 'seq', split_axis=2, concat_axis=2, tiled=True)  94.5 us
    all_to_all x1, blocking collectives, from_everyone(): return lax.all_to_all(copies, axis, split_axis=0, concat_axis=0, tiled=True)  59.7 us
    all_to_all x1, starting transfers between devices, on_device(): lax.all_to_all(outgoing, 'seq', split_axis=2, concat_axis=2, tiled=True)  5.24 us
  transfers between devices with their start and end apart: 1, of which 1 were waited for; matrix products, arithmetic and copies ran while one was open for 0% of the time, Pallas kernels for 0%

commit v1 on v0

v1 whole, which is shorter than its diff:
```python
import functools

import jax
import jax.numpy as jnp
from jax import lax
from jax.experimental import pallas as pl
from jax.experimental.pallas import tpu as pltpu
from jax.sharding import PartitionSpec as P


BLOCK = 128
epsilon = 1e-06
ceiling_value = 3e38


def build_kernel(n, count, info_ref, x_ref, *refs):
    outs, acc = refs[:-1], refs[-1]
    kinds, _, part, head = x_ref.shape
    users = info_ref.shape[0] - 1 - count
    quarter = n // users
    per_dev = quarter * part
    for u in range(users):
        live = jnp.clip(info_ref[u] - info_ref[users], 0, per_dev)
        for k in range(kinds):

            def body(b, carry):
                s, hi, lo = carry
                at = pl.multiple_of(lax.rem(b, part // BLOCK) * BLOCK, BLOCK)
                v = x_ref[k, u * quarter + b // (part // BLOCK), pl.ds(at, BLOCK), :].astype(jnp.float32)
                v = v.reshape(BLOCK // 8, 8, head)
                return s + v.sum(0), jnp.maximum(hi, v.max(0)), jnp.minimum(lo, v.min(0))

            z = jnp.zeros((8, head), jnp.float32)
            s, hi, lo = lax.fori_loop(0, live // BLOCK, body, (z, z - ceiling_value, z + ceiling_value))
            row = k * users + u
            acc[0, row:row + 1, :] = s.sum(0, keepdims=True)
            acc[1, row:row + 1, :] = hi.max(0, keepdims=True)
            acc[2, row:row + 1, :] = lo.min(0, keepdims=True)
    s = acc[0]
    p0 = s.astype(jnp.bfloat16)
    s = s - p0.astype(jnp.float32)
    p1 = s.astype(jnp.bfloat16)
    s = s - p1.astype(jnp.float32)
    p2 = s.astype(jnp.bfloat16)
    tail = jnp.concatenate([p0, p1, p2, acc[1].astype(jnp.bfloat16), acc[2].astype(jnp.bfloat16)], axis=0)
    for j in range(len(outs)):
        to = info_ref[users + 1 + j] if j < count else None

        def fill(at, j=j):
            for k in range(kinds):
                outs[j][k * part:(k + 1) * part, :] = x_ref[k, at]
            outs[j][kinds * part:, :] = tail

        if j < count:
            pl.when(to >= 0)(lambda: fill(to))
    return


def final_kernel(n, count, users, meta_ref, len_ref, *refs):
    slots = refs[:count]
    out_ref, c_ref, s_ref = refs[count], refs[count + 1], refs[count + 2]
    kinds, full, head = out_ref.shape
    part = full // n
    rows = kinds * users
    base = kinds * part
    u, first, length = meta_ref[count], meta_ref[count + 1], meta_ref[count + 2]
    per_dev = meta_ref[count + 3]
    total = jnp.zeros((rows, head), jnp.float32)
    hi = total - ceiling_value
    lo = total + ceiling_value
    for j in range(count):
        ok = meta_ref[j] >= 0
        r = slots[j]
        f = lambda i: r[base + i * rows:base + (i + 1) * rows, :].astype(jnp.float32)
        sj = (f(0) + f(1)) + f(2)
        total = total + jnp.where(ok, sj, 0.0)
        hi = jnp.maximum(hi, jnp.where(ok, f(3), -ceiling_value))
        lo = jnp.minimum(lo, jnp.where(ok, f(4), ceiling_value))
    row = lax.broadcasted_iota(jnp.int32, (rows, head), 0)
    lens = jnp.ones((rows, head), jnp.float32)
    for k in range(kinds):
        for w in range(users):
            lens = jnp.where(row == k * users + w, len_ref[w].astype(jnp.float32), lens)
    c = total / lens
    s = jnp.maximum(hi - c, c - lo) + epsilon
    c_ref[...] = c
    s_ref[...] = s
    cs = [jnp.sum(jnp.where(row == k * users + u, c, 0.0), axis=0, keepdims=True) for k in range(kinds)]
    ss = [jnp.sum(jnp.where(row == k * users + u, s, 0.0), axis=0, keepdims=True) for k in range(kinds)]
    for j in range(count):
        src = meta_ref[j]

        def put(j=j, src=src):
            pos = src * per_dev + first + lax.broadcasted_iota(jnp.int32, (part, head), 0)
            for k in range(kinds):
                v = (slots[j][k * part:(k + 1) * part, :].astype(jnp.float32) - cs[k]) / ss[k]
                v = jnp.where(pos < length, v, 0.0).astype(jnp.bfloat16)
                out_ref[k, pl.ds(pl.multiple_of(src * part, part), part), :] = v

        pl.when(src >= 0)(put)


def build_one(n, info_ref, x_ref, out, acc):
    build_kernel(n, n, info_ref, x_ref, *[out.at[j] for j in range(n)], None, acc)


def final_one(n, users, meta_ref, len_ref, got, *refs):
    final_kernel(n, n, users, meta_ref, len_ref, *[got.at[j] for j in range(n)], *refs)


def on_device(kv_cache, valid_blocks):
    kinds, _, users, per_dev, _, head = kv_cache.shape
    n = lax.axis_size("seq")
    quarter = n // users
    part = per_dev // quarter
    me = lax.axis_index("seq")
    lengths = valid_blocks.astype(jnp.int32) * BLOCK
    to = src = jnp.arange(n, dtype=jnp.int32)
    parts = kv_cache.reshape(kinds, n, part, head)
    tall = kinds * part + 5 * kinds * users
    info = jnp.concatenate([lengths, (me * per_dev)[None], to])
    sent = pl.pallas_call(
        functools.partial(build_one, n),
        out_shape=jax.ShapeDtypeStruct((n, tall, head), jnp.bfloat16),
        in_specs=[pl.BlockSpec(memory_space=pltpu.SMEM), pl.BlockSpec(memory_space=pltpu.VMEM)],
        out_specs=pl.BlockSpec(memory_space=pltpu.VMEM),
        scratch_shapes=[pltpu.VMEM((3, kinds * users, head), jnp.float32)],
    )(info, parts)
    got = [lax.all_to_all(sent, "seq", split_axis=0, concat_axis=0, tiled=True)]
    u, q = me // quarter, lax.rem(me, quarter)
    meta = jnp.concatenate([src, jnp.stack([u, q * part, lengths[u], jnp.int32(per_dev)])])
    out, centers, scales = pl.pallas_call(
        functools.partial(final_one, n, users),
        out_shape=[
            jax.ShapeDtypeStruct((kinds, n * part, head), jnp.bfloat16),
            jax.ShapeDtypeStruct((kinds * users, head), jnp.float32),
            jax.ShapeDtypeStruct((kinds * users, head), jnp.float32),
        ],
        in_specs=[pl.BlockSpec(memory_space=pltpu.SMEM)] * 2 + [pl.BlockSpec(memory_space=pltpu.VMEM)],
        out_specs=[pl.BlockSpec(memory_space=pltpu.VMEM)] * 3,
    )(meta, lengths, *got)
    return (
        out.reshape(kinds, 1, 1, n * part, 1, head),
        centers.reshape(kinds, 1, users, 1, head),
        scales.reshape(kinds, 1, users, 1, head),
    )


def solution(mesh):
    in_specs = (P(None, "layer", "groups", "seq", "head", None), P("groups"))
    out_specs = (
        P(None, "layer", ("groups", "seq"), None, "head", None),
        P(None, "layer", "groups", "head", None),
        P(None, "layer", "groups", "head", None),
    )
    return jax.shard_map(on_device, mesh=mesh, in_specs=in_specs, out_specs=out_specs, check_vma=False)
```

time: 169 us -> 157 us (0.929)
  blocking collectives: 59.7 us -> 0 us
  starting transfers between devices: 5.24 us -> 42.5 us
  Pallas kernels: 0 us -> 8.92 us
  waiting for transfers between devices: 94.5 us -> 101 us
  other arithmetic: 5.83 us -> 1.25 us
    all_to_all x1 -> x0, blocking collectives: 59.7 us -> none  [from_everyone(): return lax.all_to_all(copies, axis, split_axis=0, concat_axis=0, tiled=True)]
    all_to_all x1, starting transfers between devices: 5.24 us -> 42.5 us  [on_device(): got = [lax.all_to_all(sent, 'seq', split_axis=0, concat_axis=0, tiled=True)]]
    pallas_call x0 -> x2, Pallas kernels: none -> 8.92 us  [the longest x1 4.96 us: on_device(): pl.pallas_call(functools.partial(build_one, n), out_shape=jax.ShapeDtypeS...]
    all_to_all x1, waiting for transfers between devices: 94.5 us -> 101 us  [on_device(): got = [lax.all_to_all(sent, 'seq', split_axis=0, concat_axis=0, tiled=True)]]
    reduce_sum x1 -> x0, other arithmetic: 3.11 us -> none  [on_device(): local_sum = jnp.sum(jnp.where(live_mask, values, 0.0), axis=3)]
    convert_element_type x2 -> x0, other arithmetic: 1.81 us -> none  [the longest x1 1.01 us: on_device(): normed = jnp.where(live_mask, (values - centers[:, :, :, None]) / scales[...]
  transfers between devices with their start and end apart: 1 -> 1, of which waited for: 1 -> 1; matrix products, arithmetic and copies ran while one was open for 0% -> 1% of each run, Pallas kernels for 0% -> 0%
where the time goes in v1:
time: 157 us
  waiting for transfers between devices  101 us (64%)
  starting transfers between devices  42.5 us (27%)
  Pallas kernels  8.92 us (6%)
  local copies, waits for them, and re-layouts  3.22 us (2%)
    all_to_all x1, waiting for transfers between devices, on_device(): got = [lax.all_to_all(sent, 'seq', split_axis=0, concat_axis=0, tiled=True)]  101 us
    all_to_all x1, starting transfers between devices, on_device(): got = [lax.all_to_all(sent, 'seq', split_axis=0, concat_axis=0, tiled=True)]  42.5 us
    pallas_call x1, Pallas kernels, on_device(): pl.pallas_call(functools.partial(build_one, n), out_shape=jax.ShapeDtypeS...  4.96 us
    pallas_call x1, Pallas kernels, on_device(): pl.pallas_call(functools.partial(final_one, n, users), out_shape=[jax.Sha...  3.96 us
  transfers between devices with their start and end apart: 1, of which 1 were waited for; matrix products, arithmetic and copies ran while one was open for 1% of the time, Pallas kernels for 0%

profile of v1, /device:TPU:78, one launch (start us, length us, event | category | flops | bytes accessed | tf_op | source)
XLA Modules:
  0.0 157.0 jit_solution(10197659402204206558)
XLA Ops:
  0.6 0.7 broadcast_multiply_fusion.len_ref
  1.3 0.0 copy-start.1
  1.3 0.6 pad_add_fusion.info_ref
  1.9 5.0 %shard_map.49 = bf16[16,552,128]{2,1,0:T(8,128)(2,1)} custom-call(s32[21]{0:T(128)} %pad_add_fusion.info_ref, bf16[2,16,256,128]{3,2,1,0:T(8,128)(2,1)} %bitcast.13), custom_call_target="tpu_custom_call" | custom-call | tf_op jit(solution)/shard_map/pallas_call | solution.py:122
  6.8 42.5 %all-to-all-start = ((bf16[16,552,128]{2,1,0:T(8,128)(2,1)}), bf16[16,552,128]{2,1,0:T(8,128)(2,1)S(1)}, u32[]{:S(2)}, u32[]{:S(2)}) async-start(bf16[16,552,128]{2,1,0:T(8,128)(2,1)} %shard_map.49), calls=%async_computation | async-start | bytes 4521984 | tf_op jit(solution)/shard_map/all_to_all | solution.py:129
  49.3 0.0 copy-done.1
  49.3 0.6 dynamic_slice.3
  49.9 1.2 concatenate.6.meta_ref
  51.2 100.5 %all-to-all-done.got = bf16[16,552,128]{2,1,0:T(8,128)(2,1)S(1)} async-done(((bf16[16,552,128]{2,1,0:T(8,128)(2,1)}), bf16[16,552,128]{2,1,0:T(8,128)(2,1)S(1)}, u32[]{:S(2)}, u32[]{:S(2)}) %all-to-all-start) | async-done | bytes 2261024 | tf_op jit(solution)/shard_map/all_to_all | solution.py:129
  151.7 0.0 copy-start
  151.7 1.4 copy-done
  153.1 4.0 %shard_map.50 = (bf16[2,4096,128]{2,1,0:T(8,128)(2,1)}, f32[8,128]{1,0:T(8,128)}, f32[8,128]{1,0:T(8,128)}) custom-call(s32[20]{0:T(128)} %concatenate.6.meta_ref, s32[4]{0:T(128)} %copy-done.1, bf16[16,552,128]{2,1,0:T(8,128)(2,1)} %copy-done), custom_call_target="tpu_custom_call" | custom-call | tf_op jit(solution)/shard_map/pallas_call | solution.py:132
  (2 shorter events, 0.0 us)
Async XLA Ops:
  1.3 48.0 %copy-start.1 = (s32[4]{0:T(128)}, s32[4]{0:T(128)S(1)}, u32[]{:S(2)}) copy-start(s32[4]{0:T(128)S(1)} %broadcast_multiply_fusion.len_ref) | copy-start | bytes 52
  6.8 144.8 %all-to-all-start = ((bf16[16,552,128]{2,1,0:T(8,128)(2,1)}), bf16[16,552,128]{2,1,0:T(8,128)(2,1)S(1)}, u32[]{:S(2)}, u32[]{:S(2)}) async-start(bf16[16,552,128]{2,1,0:T(8,128)(2,1)} %shard_map.49), calls=%async_computation | async-start | bytes 4521984 | tf_op jit(solution)/shard_map/all_to_all | solution.py:129
  151.7 1.4 copy-start

commit v2 on v1

v2 whole, which is shorter than its diff:
```python
import functools

import jax
import jax.numpy as jnp
from jax import lax
from jax.experimental import pallas as pl
from jax.experimental.pallas import tpu as pltpu
from jax.sharding import PartitionSpec as P

BLOCK = 128
epsilon = 1e-06
ceiling_value = 3e38
LIMIT = 16 << 20


def live_blocks(blocks, src, per_dev):
    return jnp.clip(blocks - src * (per_dev // BLOCK), 0, per_dev // BLOCK)


def build_kernel(vb_ref, x_hbm, slots, acc, sems):
    kinds, users, _, head = x_hbm.shape
    n = slots.shape[0]
    per_dev = x_hbm.shape[2]
    quarter = n // users
    part = per_dev // quarter
    rows = kinds * users
    per = part // BLOCK
    me = lax.axis_index("seq")
    loads = {}
    for u in range(users):
        for k in range(kinds):
            for q in range(quarter):
                c = pltpu.make_async_copy(
                    x_hbm.at[k, u, pl.ds(q * part, part)],
                    slots.at[u * quarter + q, pl.ds(k * part, part)],
                    sems.at[k * users + u, q],
                )
                loads[k, u, q] = c
    alive = {
        (u, q): live_blocks(vb_ref[u], me, per_dev) > q * per for u in range(users) for q in range(quarter)
    }
    for (k, u, q), c in loads.items():
        pl.when(alive[u, q])(c.start)
    for u in range(users):
        live = live_blocks(vb_ref[u], me, per_dev)
        for k in range(kinds):
            for q in range(quarter):
                pl.when(alive[u, q])(loads[k, u, q].wait)

            def body(b, carry):
                s, hi, lo = carry
                at = pl.multiple_of(k * part + lax.rem(b, per) * BLOCK, BLOCK)
                v = slots[u * quarter + b // per, pl.ds(at, BLOCK), :].astype(jnp.float32)
                v = v.reshape(BLOCK // 8, 8, head)
                return s + v.sum(0), jnp.maximum(hi, v.max(0)), jnp.minimum(lo, v.min(0))

            z = jnp.zeros((8, head), jnp.float32)
            s, hi, lo = lax.fori_loop(0, live, body, (z, z - ceiling_value, z + ceiling_value))
            row = k * users + u
            hi = hi.max(0, keepdims=True)
            lo = lo.min(0, keepdims=True)
            count = (live * BLOCK).astype(jnp.float32)
            acc[0, row:row + 1, :] = s.sum(0, keepdims=True) - count * ((hi + lo) * 0.5)
            acc[1, row:row + 1, :] = hi
            acc[2, row:row + 1, :] = lo
    first = acc[0].astype(jnp.bfloat16)
    second = (acc[0] - first.astype(jnp.float32)).astype(jnp.bfloat16)
    tail = jnp.concatenate([first, second, acc[1].astype(jnp.bfloat16), acc[2].astype(jnp.bfloat16)], axis=0)
    for t in range(n):
        slots[t, kinds * part:, :] = tail


def final_kernel(vb_ref, slots, out_hbm, c_ref, s_ref, out_ref, acc, sems):
    kinds, full, head = out_ref.shape
    n = slots.shape[0]
    part = full // n
    users = vb_ref.shape[0]
    quarter = n // users
    per_dev = part * quarter
    rows = kinds * users
    base = kinds * part
    me = lax.axis_index("seq")
    u, q = me // quarter, lax.rem(me, quarter)
    row = lax.broadcasted_iota(jnp.int32, (rows, head), 0)

    def by_row(values):
        out = jnp.zeros((rows, head), jnp.float32)
        for k in range(kinds):
            for w in range(users):
                out = jnp.where(row == k * users + w, values[w].astype(jnp.float32), out)
        return out

    def read(src, i):
        return slots[src, base + i * rows:base + (i + 1) * rows, :].astype(jnp.float32)

    blocks = by_row([vb_ref[w] for w in range(users)])
    total = jnp.zeros((rows, head), jnp.float32)
    hi, lo = total - ceiling_value, total + ceiling_value
    for src in range(n):
        count = jnp.clip(blocks - src * (per_dev // BLOCK), 0, per_dev // BLOCK) * BLOCK
        top, bottom = read(src, 2), read(src, 3)
        total = total + ((read(src, 0) + read(src, 1)) + count * ((top + bottom) * 0.5))
        hi = jnp.maximum(hi, top)
        lo = jnp.minimum(lo, bottom)
    c = total / (blocks * BLOCK)
    s = jnp.maximum(hi - c, c - lo) + epsilon
    c_ref[...] = c
    s_ref[...] = s
    acc[0] = c
    acc[1] = s
    cs = [acc[0, pl.ds(k * users + u, 1), :] for k in range(kinds)]
    ss = [acc[1, pl.ds(k * users + u, 1), :] for k in range(kinds)]
    blocks_here = vb_ref[u]

    def copy(k, src):
        at = pl.ds(pl.multiple_of(src * part, part), part)
        return pltpu.make_async_copy(out_ref.at[k, at], out_hbm.at[k, at], sems.at[k])

    def one(src, _):
        for b in range(part // BLOCK):
            live = src * (per_dev // BLOCK) + q * (part // BLOCK) + b < blocks_here
            at = pl.multiple_of(src * part + b * BLOCK, BLOCK)

            @pl.when(live)
            def _():
                for k in range(kinds):
                    v = slots[src, k * part + b * BLOCK:k * part + (b + 1) * BLOCK, :].astype(jnp.float32)
                    out_ref[k, pl.ds(at, BLOCK), :] = ((v - cs[k]) / ss[k]).astype(jnp.bfloat16)

            @pl.when(jnp.logical_not(live))
            def _():
                for k in range(kinds):
                    out_ref[k, pl.ds(at, BLOCK), :] = jnp.zeros((BLOCK, head), jnp.bfloat16)

        for k in range(kinds):
            copy(k, src).start()
        return 0

    lax.fori_loop(0, n, one, 0)
    for k in range(kinds):
        pltpu.make_async_copy(out_ref.at[k], out_hbm.at[k], sems.at[k]).wait()


def on_device(kv_cache, valid_blocks):
    kinds, _, users, per_dev, _, head = kv_cache.shape
    n = lax.axis_size("seq")
    part = per_dev * users // n
    rows = kinds * users
    full = n * part
    x = kv_cache.reshape(kinds, users, per_dev, head)
    tall = kinds * part + 4 * rows
    anys = pl.BlockSpec(memory_space=pl.ANY)
    vmem = pl.BlockSpec(memory_space=pltpu.VMEM)
    smem = pl.BlockSpec(memory_space=pltpu.SMEM)
    slots = pl.pallas_call(
        build_kernel,
        out_shape=pltpu.VMEM((n, tall, head), jnp.bfloat16),
        in_specs=[smem, anys],
        out_specs=vmem,
        scratch_shapes=[
            pltpu.VMEM((3, rows, head), jnp.float32),
            pltpu.SemaphoreType.DMA((rows, n // users)),
        ],
    )(valid_blocks, x)
    slots = lax.all_to_all(slots, "seq", split_axis=0, concat_axis=0, tiled=True)
    slots = pltpu.with_memory_space_constraint(slots, pltpu.VMEM)
    small = jax.ShapeDtypeStruct((rows, head), jnp.float32)
    out, centers, scales = pl.pallas_call(
        final_kernel,
        out_shape=[jax.ShapeDtypeStruct((kinds, full, head), jnp.bfloat16), small, small],
        in_specs=[smem, vmem],
        out_specs=[anys, vmem, vmem],
        scratch_shapes=[
            pltpu.VMEM((kinds, full, head), jnp.bfloat16),
            pltpu.VMEM((2, rows, head), jnp.float32),
            pltpu.SemaphoreType.DMA((kinds,)),
        ],
        compiler_params=pltpu.CompilerParams(vmem_limit_bytes=LIMIT),
    )(valid_blocks, slots)
    return (
        out.reshape(kinds, 1, 1, full, 1, head),
        centers.reshape(kinds, 1, users, 1, head),
        scales.reshape(kinds, 1, users, 1, head),
    )


def solution(mesh):
    in_specs = (P(None, "layer", "groups", "seq", "head", None), P("groups"))
    out_specs = (
        P(None, "layer", ("groups", "seq"), None, "head", None),
        P(None, "layer", "groups", "head", None),
        P(None, "layer", "groups", "head", None),
    )
    return jax.shard_map(on_device, mesh=mesh, in_specs=in_specs, out_specs=out_specs, check_vma=False)
```

time: 157 us -> 153 us (0.975)
  blocking collectives: 0 us -> 146 us
  waiting for transfers between devices: 101 us -> 0 us
  starting transfers between devices: 42.5 us -> 0 us
  local copies, waits for them, and re-layouts: 3.22 us -> 0.01 us
  Pallas kernels: 8.92 us -> 6.29 us
    all_to_all x0 -> x1, blocking collectives: none -> 146 us  [on_device(): lax.all_to_all(slots, 'seq', split_axis=0, concat_axis=0, tiled=True)]
    all_to_all x1 -> x0, waiting for transfers between devices: 101 us -> none  [on_device(): got = [lax.all_to_all(sent, 'seq', split_axis=0, concat_axis=0, tiled=True)]]
    all_to_all x1 -> x0, starting transfers between devices: 42.5 us -> none  [on_device(): got = [lax.all_to_all(sent, 'seq', split_axis=0, concat_axis=0, tiled=True)]]
    pallas_call x2, Pallas kernels: 8.92 us -> 6.29 us  [the longest x1 3.7 us: on_device(): pl.pallas_call(build_kernel, out_shape=pltpu.VMEM((n, tall, head), jnp.bf...]
  transfers between devices with their start and end apart: 1 -> 0, of which waited for: 1 -> 0; matrix products, arithmetic and copies ran while one was open for 1% -> 0% of each run, Pallas kernels for 0% -> 0%
where the time goes in v2:
time: 153 us
  blocking collectives  146 us (95%)
  Pallas kernels  6.29 us (4%)
    all_to_all x1, blocking collectives, on_device(): lax.all_to_all(slots, 'seq', split_axis=0, concat_axis=0, tiled=True)  146 us
    pallas_call x1, Pallas kernels, on_device(): pl.pallas_call(build_kernel, out_shape=pltpu.VMEM((n, tall, head), jnp.bf...  3.7 us

profile of v2, /device:TPU:78, one launch (start us, length us, event | category | flops | bytes accessed | tf_op | source)
XLA Modules:
  0.0 152.9 jit_solution(9352978372988944150)
XLA Ops:
  0.6 3.7 %shard_map.49 = bf16[16,544,128]{2,1,0:T(8,128)(2,1)S(1)} custom-call(s32[4]{0:T(128)} %vb_ref.3, bf16[2,4,1024,128]{3,2,1,0:T(8,128)(2,1)} %bitcast.10), custom_call_target="tpu_custom_call" | custom-call | tf_op jit(solution)/shard_map/pallas_call | solution.py:155
  4.3 0.0 copy-start
  4.4 146.0 %all_to_all.5.slots = bf16[16,544,128]{2,1,0:T(8,128)(2,1)S(1)} all-to-all(bf16[16,544,128]{2,1,0:T(8,128)(2,1)S(1)} %shard_map.49), channel_id=1, replica_groups=mesh['groups'=2,'seq'=16,'head'=8,'layer'=2] {'seq'}, dimensions={0} | all-to-all | bytes 4456448 | tf_op jit(solution)/shard_map/all_to_all | solution.py:165
  150.3 0.0 copy-done
  150.3 2.6 %shard_map.50 = (bf16[2,4096,128]{2,1,0:T(8,128)(2,1)}, f32[8,128]{1,0:T(8,128)}, f32[8,128]{1,0:T(8,128)}) custom-call(s32[4]{0:T(128)S(1)} %copy-done, bf16[16,544,128]{2,1,0:T(8,128)(2,1)S(1)} %all_to_all.5.slots), custom_call_target="tpu_custom_call" | custom-call | tf_op jit(solution)/shard_map/pallas_call | solution.py:168
Async XLA Ops:
  4.3 146.0 %copy-start = (s32[4]{0:T(128)S(1)}, s32[4]{0:T(128)}, u32[]{:S(2)}) copy-start(s32[4]{0:T(128)} %vb_ref.3) | copy-start | bytes 52

commit v3 on v2

v3 whole, which is shorter than its diff:
```python
import functools

import jax
import jax.numpy as jnp
from jax import lax
from jax.experimental import pallas as pl
from jax.experimental.pallas import tpu as pltpu
from jax.sharding import PartitionSpec as P


BLOCK = 128
epsilon = 1e-06
ceiling_value = 3e38
LIMIT = 16 << 20


def shifts(n):
    return [n // 2] + [s * k for k in range(n // 2 - 1, 0, -1) for s in (1, -1)]


def live_blocks(blocks, src, per_dev):
    return jnp.clip(blocks - src * (per_dev // BLOCK), 0, per_dev // BLOCK)


def build_kernel(order, vb_ref, x_hbm, *refs):
    n = len(order) + 1
    slots, (x_ref, acc, in_sems) = refs[:n], refs[n:]
    kinds, users, per_dev, head = x_hbm.shape
    quarter = n // users
    part = per_dev // quarter
    me = lax.axis_index("seq")
    live = [live_blocks(vb_ref[u], me, per_dev) for u in range(users)]
    loads = {
        (k, u): pltpu.make_async_copy(x_hbm.at[k, u], x_ref.at[k, u], in_sems.at[k, u])
        for u in range(users) for k in range(kinds)
    }
    for (k, u), c in loads.items():
        pl.when(live[u] > 0)(c.start)
    for u in range(users):
        for k in range(kinds):
            pl.when(live[u] > 0)(loads[k, u].wait)

            def body(b, carry):
                s, hi, lo = carry
                v = x_ref[k, u, pl.ds(pl.multiple_of(b * BLOCK, BLOCK), BLOCK), :].astype(jnp.float32)
                v = v.reshape(BLOCK // 8, 8, head)
                return s + v.sum(0), jnp.maximum(hi, v.max(0)), jnp.minimum(lo, v.min(0))

            z = jnp.zeros((8, head), jnp.float32)
            s, hi, lo = lax.fori_loop(0, live[u], body, (z, z - ceiling_value, z + ceiling_value))
            row = k * users + u
            hi = hi.max(0, keepdims=True)
            lo = lo.min(0, keepdims=True)
            count = (live[u] * BLOCK).astype(jnp.float32)
            acc[0, row:row + 1, :] = s.sum(0, keepdims=True) - count * ((hi + lo) * 0.5)
            acc[1, row:row + 1, :] = hi
            acc[2, row:row + 1, :] = lo
    first = acc[0].astype(jnp.bfloat16)
    second = (acc[0] - first.astype(jnp.float32)).astype(jnp.bfloat16)
    tail = jnp.concatenate([first, second, acc[1].astype(jnp.bfloat16), acc[2].astype(jnp.bfloat16)], axis=0)
    for j, shift in enumerate(list(order) + [0]):
        to = lax.rem(me + shift + n, n)
        u, q = to // quarter, lax.rem(to, quarter)
        for k in range(kinds):
            slots[j][k * part:(k + 1) * part, :] = x_ref[k, u, pl.ds(pl.multiple_of(q * part, part), part), :]
        slots[j][kinds * part:, :] = tail


def final_kernel(order, vb_ref, *refs):
    n = len(order) + 1
    slots, (out_hbm, c_ref, s_ref, out_ref, acc, sems) = refs[:n], refs[n:]
    kinds, full, head = out_ref.shape
    part = full // n
    users = vb_ref.shape[0]
    quarter = n // users
    per_dev = part * quarter
    rows = kinds * users
    base = kinds * part
    me = lax.axis_index("seq")
    u, q = me // quarter, lax.rem(me, quarter)
    row = lax.broadcasted_iota(jnp.int32, (rows, head), 0)
    blocks = jnp.zeros((rows, head), jnp.float32)
    for k in range(kinds):
        for w in range(users):
            blocks = jnp.where(row == k * users + w, vb_ref[w].astype(jnp.float32), blocks)
    source = [lax.rem(me - shift + n, n) for shift in list(order) + [0]]
    for j in range(n):
        acc[source[j]] = slots[j][base:, :].astype(jnp.float32)
    total = jnp.zeros((rows, head), jnp.float32)
    hi, lo = total - ceiling_value, total + ceiling_value
    for src in range(n):
        a, b, top, bottom = (acc[src, i * rows:(i + 1) * rows, :] for i in range(4))
        count = jnp.clip(blocks - src * (per_dev // BLOCK), 0, per_dev // BLOCK) * BLOCK
        total = total + ((a + b) + count * ((top + bottom) * 0.5))
        hi = jnp.maximum(hi, top)
        lo = jnp.minimum(lo, bottom)
    c = total / (blocks * BLOCK)
    s = jnp.maximum(hi - c, c - lo) + epsilon
    c_ref[...] = c
    s_ref[...] = s
    cs = [c_ref[pl.ds(k * users + u, 1), :] for k in range(kinds)]
    ss = [s_ref[pl.ds(k * users + u, 1), :] for k in range(kinds)]
    blocks_here = vb_ref[u]
    for j in range(n):
        src = source[j]
        for b in range(part // BLOCK):
            live = src * (per_dev // BLOCK) + q * (part // BLOCK) + b < blocks_here
            at = pl.multiple_of(src * part + b * BLOCK, BLOCK)

            @pl.when(live)
            def _():
                for k in range(kinds):
                    v = slots[j][k * part + b * BLOCK:k * part + (b + 1) * BLOCK, :].astype(jnp.float32)
                    out_ref[k, pl.ds(at, BLOCK), :] = ((v - cs[k]) / ss[k]).astype(jnp.bfloat16)

            @pl.when(jnp.logical_not(live))
            def _():
                for k in range(kinds):
                    out_ref[k, pl.ds(at, BLOCK), :] = jnp.zeros((BLOCK, head), jnp.bfloat16)

        for k in range(kinds):
            at = pl.ds(pl.multiple_of(src * part, part), part)
            pltpu.make_async_copy(out_ref.at[k, at], out_hbm.at[k, at], sems.at[k]).start()
    for k in range(kinds):
        pltpu.make_async_copy(out_ref.at[k], out_hbm.at[k], sems.at[k]).wait()


def on_device(kv_cache, valid_blocks):
    kinds, _, users, per_dev, _, head = kv_cache.shape
    n = lax.axis_size("seq")
    part = per_dev * users // n
    rows = kinds * users
    full = n * part
    order = shifts(n)
    x = kv_cache.reshape(kinds, users, per_dev, head)
    tall = kinds * part + 4 * rows
    anys = pl.BlockSpec(memory_space=pl.ANY)
    vmem = pl.BlockSpec(memory_space=pltpu.VMEM)
    smem = pl.BlockSpec(memory_space=pltpu.SMEM)
    slots = pl.pallas_call(
        functools.partial(build_kernel, order),
        out_shape=[pltpu.VMEM((tall, head), jnp.bfloat16)] * n,
        in_specs=[smem, anys],
        out_specs=[vmem] * n,
        scratch_shapes=[
            pltpu.VMEM((kinds, users, per_dev, head), jnp.bfloat16),
            pltpu.VMEM((3, rows, head), jnp.float32),
            pltpu.SemaphoreType.DMA((kinds, users)),
        ],
    )(valid_blocks, x)
    got = []
    for j, shift in enumerate(order):
        got.append(lax.ppermute(slots[j], "seq", [(s, (s + shift) % n) for s in range(n)]))
    got.append(slots[-1])
    got = [pltpu.with_memory_space_constraint(g, pltpu.VMEM) for g in got]
    small = jax.ShapeDtypeStruct((rows, head), jnp.float32)
    out, centers, scales = pl.pallas_call(
        functools.partial(final_kernel, order),
        out_shape=[jax.ShapeDtypeStruct((kinds, full, head), jnp.bfloat16), small, small],
        in_specs=[smem] + [vmem] * n,
        out_specs=[anys, vmem, vmem],
        scratch_shapes=[
            pltpu.VMEM((kinds, full, head), jnp.bfloat16),
            pltpu.VMEM((n, 4 * rows, head), jnp.float32),
            pltpu.SemaphoreType.DMA((kinds,)),
        ],
        compiler_params=pltpu.CompilerParams(vmem_limit_bytes=LIMIT),
    )(valid_blocks, *got)
    return (
        out.reshape(kinds, 1, 1, full, 1, head),
        centers.reshape(kinds, 1, users, 1, head),
        scales.reshape(kinds, 1, users, 1, head),
    )


def solution(mesh):
    in_specs = (P(None, "layer", "groups", "seq", "head", None), P("groups"))
    out_specs = (
        P(None, "layer", ("groups", "seq"), None, "head", None),
        P(None, "layer", "groups", "head", None),
        P(None, "layer", "groups", "head", None),
    )
    return jax.shard_map(on_device, mesh=mesh, in_specs=in_specs, out_specs=out_specs, check_vma=False)
```

time: 153 us -> 145 us (0.948)
  blocking collectives: 146 us -> 0 us
  starting transfers between devices: 0 us -> 126 us
  waiting for transfers between devices: 0 us -> 12 us
    all_to_all x1 -> x0, blocking collectives: 146 us -> none  [on_device(): lax.all_to_all(slots, 'seq', split_axis=0, concat_axis=0, tiled=True)]
    ppermute x0 -> x15, starting transfers between devices: none -> 126 us  [on_device(): lax.ppermute(slots[j], 'seq', [(s, (s + shift) % n) for s in range(n)])]
    ppermute x0 -> x15, waiting for transfers between devices: none -> 12 us  [on_device(): lax.ppermute(slots[j], 'seq', [(s, (s + shift) % n) for s in range(n)])]
  transfers between devices with their start and end apart: 0 -> 15, of which waited for: 0 -> 7; matrix products, arithmetic and copies ran while one was open for 0% -> 0% of each run, Pallas kernels for 0% -> 0%
where the time goes in v3:
time: 145 us
  starting transfers between devices  126 us (87%)
  waiting for transfers between devices  12 us (8%)
  Pallas kernels  5.86 us (4%)
    ppermute x15, starting transfers between devices, on_device(): lax.ppermute(slots[j], 'seq', [(s, (s + shift) % n) for s in range(n)])  126 us
    ppermute x15, waiting for transfers between devices, on_device(): lax.ppermute(slots[j], 'seq', [(s, (s + shift) % n) for s in range(n)])  12 us
    pallas_call x1, Pallas kernels, on_device(): pl.pallas_call(functools.partial(build_kernel, order), out_shape=[pltpu.V...  3.31 us
  transfers between devices with their start and end apart: 15, of which 7 were waited for; matrix products, arithmetic and copies ran while one was open for 0% of the time, Pallas kernels for 0%

profile of v3, /device:TPU:78, one launch (start us, length us, event | category | flops | bytes accessed | tf_op | source)
XLA Modules:
  0.0 144.7 jit_solution(17281357189964458967)
XLA Ops:
  0.6 3.3 %shard_map.49 = (bf16[544,128]{1,0:T(8,128)(2,1)S(1)}, bf16[544,128]{1,0:T(8,128)(2,1)S(1)}, bf16[544,128]{1,0:T(8,128)(2,1)S(1)}, bf16[544,128]{1,0:T(8,128)(2,...) custom-call(s32[4]{0:T(128)} %vb_ref.3, ...), custom_call_target="tpu_custom_call" | custom-call | tf_op jit(solution)/shard_map/pallas_call | solution.py:140
  4.0 32.3 %collective-permute-start = (bf16[544,128]{1,0:T(8,128)(2,1)S(1)}, bf16[544,128]{1,0:T(8,128)(2,1)S(1)}, u32[]{:S(2)}, u32[]{:S(2)}) collective-permute-start(bf16[544,128]{1,0:T(8,128)(2,1)S(1)} %get-tuple-element.22), channel_id=1, source_target_pairs={{0,128},{16,144},{32,160},{48,176},{64,192},{80,208},{96,224},{112... | collective-permute-start | bytes 417800 | tf_op jit(solution)/shard_map/ppermute | solution.py:153
  36.2 20.7 %collective-permute-start.1 = (bf16[544,128]{1,0:T(8,128)(2,1)S(1)}, bf16[544,128]{1,0:T(8,128)(2,1)S(1)}, u32[]{:S(2)}, u32[]{:S(2)}) collective-permute-start(bf16[544,128]{1,0:T(8,128)(2,1)S(1)} %get-tuple-element.23), channel_id=1, source_target_pairs={{0,112},{16,128},{32,144},{48,160},{64,176},{80,192},{96,208},{112... | collective-permute-start | bytes 417800 | tf_op jit(solution)/shard_map/ppermute | solution.py:153
  57.0 2.0 %collective-permute-start.2 = (bf16[544,128]{1,0:T(8,128)(2,1)S(1)}, bf16[544,128]{1,0:T(8,128)(2,1)S(1)}, u32[]{:S(2)}, u32[]{:S(2)}) collective-permute-start(bf16[544,128]{1,0:T(8,128)(2,1)S(1)} %get-tuple-element.24), channel_id=1, source_target_pairs={{0,144},{16,160},{32,176},{48,192},{64,208},{80,224},{96,240},{112... | collective-permute-start | bytes 417800 | tf_op jit(solution)/shard_map/ppermute | solution.py:153
  58.9 9.1 %collective-permute-start.3 = (bf16[544,128]{1,0:T(8,128)(2,1)S(1)}, bf16[544,128]{1,0:T(8,128)(2,1)S(1)}, u32[]{:S(2)}, u32[]{:S(2)}) collective-permute-start(bf16[544,128]{1,0:T(8,128)(2,1)S(1)} %get-tuple-element.25), channel_id=1, source_target_pairs={{0,96},{16,112},{32,128},{48,144},{64,160},{80,176},{96,192},{112,... | collective-permute-start | bytes 417800 | tf_op jit(solution)/shard_map/ppermute | solution.py:153
  68.1 3.7 %collective-permute-start.4 = (bf16[544,128]{1,0:T(8,128)(2,1)S(1)}, bf16[544,128]{1,0:T(8,128)(2,1)S(1)}, u32[]{:S(2)}, u32[]{:S(2)}) collective-permute-start(bf16[544,128]{1,0:T(8,128)(2,1)S(1)} %get-tuple-element.26), channel_id=1, source_target_pairs={{0,160},{16,176},{32,192},{48,208},{64,224},{80,240},{96,0},{112,1... | collective-permute-start | bytes 417800 | tf_op jit(solution)/shard_map/ppermute | solution.py:153
  71.8 0.0 collective-permute-done.refs_0_
  71.8 6.5 %collective-permute-start.5 = (bf16[544,128]{1,0:T(8,128)(2,1)S(1)}, bf16[544,128]{1,0:T(8,128)(2,1)S(1)}, u32[]{:S(2)}, u32[]{:S(2)}) collective-permute-start(bf16[544,128]{1,0:T(8,128)(2,1)S(1)} %get-tuple-element.27), channel_id=1, source_target_pairs={{0,80},{16,96},{32,112},{48,128},{64,144},{80,160},{96,176},{112,1... | collective-permute-start | bytes 417800 | tf_op jit(solution)/shard_map/ppermute | solution.py:153
  78.3 5.2 %collective-permute-done.1.refs_1_ = bf16[544,128]{1,0:T(8,128)(2,1)S(1)} collective-permute-done((bf16[544,128]{1,0:T(8,128)(2,1)S(1)}, bf16[544,128]{1,0:T(8,128)(2,1)S(1)}, u32[]{:S(2)}, u32[]{:S(2)}) %collective-permute-start.1) | collective-permute-done | bytes 139296 | tf_op jit(solution)/shard_map/ppermute | solution.py:153
  83.5 3.0 %collective-permute-start.6 = (bf16[544,128]{1,0:T(8,128)(2,1)S(1)}, bf16[544,128]{1,0:T(8,128)(2,1)S(1)}, u32[]{:S(2)}, u32[]{:S(2)}) collective-permute-start(bf16[544,128]{1,0:T(8,128)(2,1)S(1)} %get-tuple-element.28), channel_id=1, source_target_pairs={{0,176},{16,192},{32,208},{48,224},{64,240},{80,0},{96,16},{112,32... | collective-permute-start | bytes 417800 | tf_op jit(solution)/shard_map/ppermute | solution.py:153
  86.5 0.0 collective-permute-done.2.refs_2_
  86.5 13.9 %collective-permute-start.7 = (bf16[544,128]{1,0:T(8,128)(2,1)S(1)}, bf16[544,128]{1,0:T(8,128)(2,1)S(1)}, u32[]{:S(2)}, u32[]{:S(2)}) collective-permute-start(bf16[544,128]{1,0:T(8,128)(2,1)S(1)} %get-tuple-element.29), channel_id=1, source_target_pairs={{0,64},{16,80},{32,96},{48,112},{64,128},{80,144},{96,160},{112,17... | collective-permute-start | bytes 417800 | tf_op jit(solution)/shard_map/ppermute | solution.py:153
  100.5 0.7 collective-permute-done.3.refs_3_
  101.2 6.4 %collective-permute-start.8 = (bf16[544,128]{1,0:T(8,128)(2,1)S(1)}, bf16[544,128]{1,0:T(8,128)(2,1)S(1)}, u32[]{:S(2)}, u32[]{:S(2)}) collective-permute-start(bf16[544,128]{1,0:T(8,128)(2,1)S(1)} %get-tuple-element.30), channel_id=1, source_target_pairs={{0,192},{16,208},{32,224},{48,240},{64,0},{80,16},{96,32},{112,48}... | collective-permute-start | bytes 417800 | tf_op jit(solution)/shard_map/ppermute | solution.py:153
  107.6 0.0 collective-permute-done.4.refs_4_
  107.6 2.0 %collective-permute-start.9 = (bf16[544,128]{1,0:T(8,128)(2,1)S(1)}, bf16[544,128]{1,0:T(8,128)(2,1)S(1)}, u32[]{:S(2)}, u32[]{:S(2)}) collective-permute-start(bf16[544,128]{1,0:T(8,128)(2,1)S(1)} %get-tuple-element.31), channel_id=1, source_target_pairs={{0,48},{16,64},{32,80},{48,96},{64,112},{80,128},{96,144},{112,160... | collective-permute-start | bytes 417800 | tf_op jit(solution)/shard_map/ppermute | solution.py:153
  109.5 0.0 collective-permute-done.5.refs_5_
  109.6 7.0 %collective-permute-start.10 = (bf16[544,128]{1,0:T(8,128)(2,1)S(1)}, bf16[544,128]{1,0:T(8,128)(2,1)S(1)}, u32[]{:S(2)}, u32[]{:S(2)}) collective-permute-start(bf16[544,128]{1,0:T(8,128)(2,1)S(1)} %get-tuple-element.32), channel_id=1, source_target_pairs={{0,208},{16,224},{32,240},{48,0},{64,16},{80,32},{96,48},{112,64},... | collective-permute-start | bytes 417800 | tf_op jit(solution)/shard_map/ppermute | solution.py:153
  116.5 0.3 collective-permute-done.6.refs_6_
  116.8 4.0 %collective-permute-start.11 = (bf16[544,128]{1,0:T(8,128)(2,1)S(1)}, bf16[544,128]{1,0:T(8,128)(2,1)S(1)}, u32[]{:S(2)}, u32[]{:S(2)}) collective-permute-start(bf16[544,128]{1,0:T(8,128)(2,1)S(1)} %get-tuple-element.33), channel_id=1, source_target_pairs={{0,32},{16,48},{32,64},{48,80},{64,96},{80,112},{96,128},{112,144}... | collective-permute-start | bytes 417800 | tf_op jit(solution)/shard_map/ppermute | solution.py:153
  120.8 1.8 %collective-permute-done.7.refs_7_ = bf16[544,128]{1,0:T(8,128)(2,1)S(1)} collective-permute-done((bf16[544,128]{1,0:T(8,128)(2,1)S(1)}, bf16[544,128]{1,0:T(8,128)(2,1)S(1)}, u32[]{:S(2)}, u32[]{:S(2)}) %collective-permute-start.7) | collective-permute-done | bytes 139296 | tf_op jit(solution)/shard_map/ppermute | solution.py:153
  122.6 2.3 %collective-permute-start.12 = (bf16[544,128]{1,0:T(8,128)(2,1)S(1)}, bf16[544,128]{1,0:T(8,128)(2,1)S(1)}, u32[]{:S(2)}, u32[]{:S(2)}) collective-permute-start(bf16[544,128]{1,0:T(8,128)(2,1)S(1)} %get-tuple-element.34), channel_id=1, source_target_pairs={{0,224},{16,240},{32,0},{48,16},{64,32},{80,48},{96,64},{112,80},{... | collective-permute-start | bytes 417800 | tf_op jit(solution)/shard_map/ppermute | solution.py:153
  124.9 0.0 collective-permute-done.8.refs_8_
  124.9 5.0 %collective-permute-start.13 = (bf16[544,128]{1,0:T(8,128)(2,1)S(1)}, bf16[544,128]{1,0:T(8,128)(2,1)S(1)}, u32[]{:S(2)}, u32[]{:S(2)}) collective-permute-start(bf16[544,128]{1,0:T(8,128)(2,1)S(1)} %get-tuple-element.35), channel_id=1, source_target_pairs={{0,16},{16,32},{32,48},{48,64},{64,80},{80,96},{96,112},{112,128},... | collective-permute-start | bytes 417800 | tf_op jit(solution)/shard_map/ppermute | solution.py:153
  129.9 0.0 collective-permute-done.9.refs_9_
  129.9 8.3 %collective-permute-start.14 = (bf16[544,128]{1,0:T(8,128)(2,1)S(1)}, bf16[544,128]{1,0:T(8,128)(2,1)S(1)}, u32[]{:S(2)}, u32[]{:S(2)}) collective-permute-start(bf16[544,128]{1,0:T(8,128)(2,1)S(1)} %get-tuple-element.36), channel_id=1, source_target_pairs={{0,240},{16,0},{32,16},{48,32},{64,48},{80,64},{96,80},{112,96},{1... | collective-permute-start | bytes 417800 | tf_op jit(solution)/shard_map/ppermute | solution.py:153
  138.2 0.1 collective-permute-done.10.refs_10_
  138.3 0.0 collective-permute-done.11.refs_11_
  138.3 0.0 collective-permute-done.12.refs_12_
  138.3 0.9 collective-permute-done.13.refs_13_
  139.2 2.9 %collective-permute-done.14.refs_14_ = bf16[544,128]{1,0:T(8,128)(2,1)S(1)} collective-permute-done((bf16[544,128]{1,0:T(8,128)(2,1)S(1)}, bf16[544,128]{1,0:T(8,128)(2,1)S(1)}, u32[]{:S(2)}, u32[]{:S(2)}) %collective-permute-start.14) | collective-permute-done | bytes 139296 | tf_op jit(solution)/shard_map/ppermute | solution.py:153
  142.2 2.6 %shard_map.50 = (bf16[2,4096,128]{2,1,0:T(8,128)(2,1)}, f32[8,128]{1,0:T(8,128)}, f32[8,128]{1,0:T(8,128)}) custom-call(s32[4]{0:T(128)S(1)} %copy-done, bf16[544,128]{1,0:T(8,128)(2,1)S(1)} %collective-permute-done.refs_0_, bf16[544,128]{1,0:T(8,128)(2,1)S(1)} %collective-permute-done.1.refs_1_, bf16[544,128]{1,0:T(8,128)(2,1)S(1)} %collective-permute-done.2.refs_2_, ...), custom_call_target="tpu_custom_call" | custom-call | tf_op jit(solution)/shard_map/pallas_call | solution.py:157
  (2 shorter events, 0.0 us)
Async XLA Ops:
  0.6 141.6 %copy-start = (s32[4]{0:T(128)S(1)}, s32[4]{0:T(128)}, u32[]{:S(2)}) copy-start(s32[4]{0:T(128)} %vb_ref.3) | copy-start | bytes 52
  4.0 67.8 %collective-permute-start = (bf16[544,128]{1,0:T(8,128)(2,1)S(1)}, bf16[544,128]{1,0:T(8,128)(2,1)S(1)}, u32[]{:S(2)}, u32[]{:S(2)}) collective-permute-start(bf16[544,128]{1,0:T(8,128)(2,1)S(1)} %get-tuple-element.22), channel_id=1, source_target_pairs={{0,128},{16,144},{32,160},{48,176},{64,192},{80,208},{96,224},{112... | collective-permute-start | bytes 417800 | tf_op jit(solution)/shard_map/ppermute | solution.py:153
  36.2 47.2 %collective-permute-start.1 = (bf16[544,128]{1,0:T(8,128)(2,1)S(1)}, bf16[544,128]{1,0:T(8,128)(2,1)S(1)}, u32[]{:S(2)}, u32[]{:S(2)}) collective-permute-start(bf16[544,128]{1,0:T(8,128)(2,1)S(1)} %get-tuple-element.23), channel_id=1, source_target_pairs={{0,112},{16,128},{32,144},{48,160},{64,176},{80,192},{96,208},{112... | collective-permute-start | bytes 417800 | tf_op jit(solution)/shard_map/ppermute | solution.py:153
  57.0 29.5 %collective-permute-start.2 = (bf16[544,128]{1,0:T(8,128)(2,1)S(1)}, bf16[544,128]{1,0:T(8,128)(2,1)S(1)}, u32[]{:S(2)}, u32[]{:S(2)}) collective-permute-start(bf16[544,128]{1,0:T(8,128)(2,1)S(1)} %get-tuple-element.24), channel_id=1, source_target_pairs={{0,144},{16,160},{32,176},{48,192},{64,208},{80,224},{96,240},{112... | collective-permute-start | bytes 417800 | tf_op jit(solution)/shard_map/ppermute | solution.py:153
  58.9 42.3 %collective-permute-start.3 = (bf16[544,128]{1,0:T(8,128)(2,1)S(1)}, bf16[544,128]{1,0:T(8,128)(2,1)S(1)}, u32[]{:S(2)}, u32[]{:S(2)}) collective-permute-start(bf16[544,128]{1,0:T(8,128)(2,1)S(1)} %get-tuple-element.25), channel_id=1, source_target_pairs={{0,96},{16,112},{32,128},{48,144},{64,160},{80,176},{96,192},{112,... | collective-permute-start | bytes 417800 | tf_op jit(solution)/shard_map/ppermute | solution.py:153
  68.1 39.5 %collective-permute-start.4 = (bf16[544,128]{1,0:T(8,128)(2,1)S(1)}, bf16[544,128]{1,0:T(8,128)(2,1)S(1)}, u32[]{:S(2)}, u32[]{:S(2)}) collective-permute-start(bf16[544,128]{1,0:T(8,128)(2,1)S(1)} %get-tuple-element.26), channel_id=1, source_target_pairs={{0,160},{16,176},{32,192},{48,208},{64,224},{80,240},{96,0},{112,1... | collective-permute-start | bytes 417800 | tf_op jit(solution)/shard_map/ppermute | solution.py:153
  71.8 37.8 %collective-permute-start.5 = (bf16[544,128]{1,0:T(8,128)(2,1)S(1)}, bf16[544,128]{1,0:T(8,128)(2,1)S(1)}, u32[]{:S(2)}, u32[]{:S(2)}) collective-permute-start(bf16[544,128]{1,0:T(8,128)(2,1)S(1)} %get-tuple-element.27), channel_id=1, source_target_pairs={{0,80},{16,96},{32,112},{48,128},{64,144},{80,160},{96,176},{112,1... | collective-permute-start | bytes 417800 | tf_op jit(solution)/shard_map/ppermute | solution.py:153
  83.5 33.4 %collective-permute-start.6 = (bf16[544,128]{1,0:T(8,128)(2,1)S(1)}, bf16[544,128]{1,0:T(8,128)(2,1)S(1)}, u32[]{:S(2)}, u32[]{:S(2)}) collective-permute-start(bf16[544,128]{1,0:T(8,128)(2,1)S(1)} %get-tuple-element.28), channel_id=1, source_target_pairs={{0,176},{16,192},{32,208},{48,224},{64,240},{80,0},{96,16},{112,32... | collective-permute-start | bytes 417800 | tf_op jit(solution)/shard_map/ppermute | solution.py:153
  86.5 36.1 %collective-permute-start.7 = (bf16[544,128]{1,0:T(8,128)(2,1)S(1)}, bf16[544,128]{1,0:T(8,128)(2,1)S(1)}, u32[]{:S(2)}, u32[]{:S(2)}) collective-permute-start(bf16[544,128]{1,0:T(8,128)(2,1)S(1)} %get-tuple-element.29), channel_id=1, source_target_pairs={{0,64},{16,80},{32,96},{48,112},{64,128},{80,144},{96,160},{112,17... | collective-permute-start | bytes 417800 | tf_op jit(solution)/shard_map/ppermute | solution.py:153
  101.2 23.7 %collective-permute-start.8 = (bf16[544,128]{1,0:T(8,128)(2,1)S(1)}, bf16[544,128]{1,0:T(8,128)(2,1)S(1)}, u32[]{:S(2)}, u32[]{:S(2)}) collective-permute-start(bf16[544,128]{1,0:T(8,128)(2,1)S(1)} %get-tuple-element.30), channel_id=1, source_target_pairs={{0,192},{16,208},{32,224},{48,240},{64,0},{80,16},{96,32},{112,48}... | collective-permute-start | bytes 417800 | tf_op jit(solution)/shard_map/ppermute | solution.py:153
  107.6 22.3 %collective-permute-start.9 = (bf16[544,128]{1,0:T(8,128)(2,1)S(1)}, bf16[544,128]{1,0:T(8,128)(2,1)S(1)}, u32[]{:S(2)}, u32[]{:S(2)}) collective-permute-start(bf16[544,128]{1,0:T(8,128)(2,1)S(1)} %get-tuple-element.31), channel_id=1, source_target_pairs={{0,48},{16,64},{32,80},{48,96},{64,112},{80,128},{96,144},{112,160... | collective-permute-start | bytes 417800 | tf_op jit(solution)/shard_map/ppermute | solution.py:153
  109.6 28.7 %collective-permute-start.10 = (bf16[544,128]{1,0:T(8,128)(2,1)S(1)}, bf16[544,128]{1,0:T(8,128)(2,1)S(1)}, u32[]{:S(2)}, u32[]{:S(2)}) collective-permute-start(bf16[544,128]{1,0:T(8,128)(2,1)S(1)} %get-tuple-element.32), channel_id=1, source_target_pairs={{0,208},{16,224},{32,240},{48,0},{64,16},{80,32},{96,48},{112,64},... | collective-permute-start | bytes 417800 | tf_op jit(solution)/shard_map/ppermute | solution.py:153
  116.8 21.5 %collective-permute-start.11 = (bf16[544,128]{1,0:T(8,128)(2,1)S(1)}, bf16[544,128]{1,0:T(8,128)(2,1)S(1)}, u32[]{:S(2)}, u32[]{:S(2)}) collective-permute-start(bf16[544,128]{1,0:T(8,128)(2,1)S(1)} %get-tuple-element.33), channel_id=1, source_target_pairs={{0,32},{16,48},{32,64},{48,80},{64,96},{80,112},{96,128},{112,144}... | collective-permute-start | bytes 417800 | tf_op jit(solution)/shard_map/ppermute | solution.py:153
  122.6 15.7 %collective-permute-start.12 = (bf16[544,128]{1,0:T(8,128)(2,1)S(1)}, bf16[544,128]{1,0:T(8,128)(2,1)S(1)}, u32[]{:S(2)}, u32[]{:S(2)}) collective-permute-start(bf16[544,128]{1,0:T(8,128)(2,1)S(1)} %get-tuple-element.34), channel_id=1, source_target_pairs={{0,224},{16,240},{32,0},{48,16},{64,32},{80,48},{96,64},{112,80},{... | collective-permute-start | bytes 417800 | tf_op jit(solution)/shard_map/ppermute | solution.py:153
  124.9 14.4 %collective-permute-start.13 = (bf16[544,128]{1,0:T(8,128)(2,1)S(1)}, bf16[544,128]{1,0:T(8,128)(2,1)S(1)}, u32[]{:S(2)}, u32[]{:S(2)}) collective-permute-start(bf16[544,128]{1,0:T(8,128)(2,1)S(1)} %get-tuple-element.35), channel_id=1, source_target_pairs={{0,16},{16,32},{32,48},{48,64},{64,80},{80,96},{96,112},{112,128},... | collective-permute-start | bytes 417800 | tf_op jit(solution)/shard_map/ppermute | solution.py:153
  129.9 12.3 %collective-permute-start.14 = (bf16[544,128]{1,0:T(8,128)(2,1)S(1)}, bf16[544,128]{1,0:T(8,128)(2,1)S(1)}, u32[]{:S(2)}, u32[]{:S(2)}) collective-permute-start(bf16[544,128]{1,0:T(8,128)(2,1)S(1)} %get-tuple-element.36), channel_id=1, source_target_pairs={{0,240},{16,0},{32,16},{48,32},{64,48},{80,64},{96,80},{112,96},{1... | collective-permute-start | bytes 417800 | tf_op jit(solution)/shard_map/ppermute | solution.py:153

commit v4 on v3

--- a/solution.py
+++ b/solution.py
@@ -11,11 +11,13 @@
 BLOCK = 128
 epsilon = 1e-06
 ceiling_value = 3e38
+PIECES = 2
 LIMIT = 16 << 20
 
 
 def shifts(n):
-    return [n // 2] + [s * k for k in range(n // 2 - 1, 0, -1) for s in (1, -1)]
+    pairs = [(k, -k) if k % 2 else (-k, k) for k in range(n // 2 - 1, 0, -1)]
+    return [n // 2] + [k for pair in pairs for k in pair]
 
 
 def live_blocks(blocks, src, per_dev):
@@ -49,20 +51,23 @@
             z = jnp.zeros((8, head), jnp.float32)
             s, hi, lo = lax.fori_loop(0, live[u], body, (z, z - ceiling_value, z + ceiling_value))
             row = k * users + u
-            hi = hi.max(0, keepdims=True)
-            lo = lo.min(0, keepdims=True)
-            count = (live[u] * BLOCK).astype(jnp.float32)
-            acc[0, row:row + 1, :] = s.sum(0, keepdims=True) - count * ((hi + lo) * 0.5)
-            acc[1, row:row + 1, :] = hi
-            acc[2, row:row + 1, :] = lo
-    first = acc[0].astype(jnp.bfloat16)
-    second = (acc[0] - first.astype(jnp.float32)).astype(jnp.bfloat16)
-    tail = jnp.concatenate([first, second, acc[1].astype(jnp.bfloat16), acc[2].astype(jnp.bfloat16)], axis=0)
+            acc[0, row:row + 1, :] = s.sum(0, keepdims=True)
+            acc[1, row:row + 1, :] = hi.max(0, keepdims=True)
+            acc[2, row:row + 1, :] = lo.min(0, keepdims=True)
+    rest, pieces = acc[0], []
+    for _ in range(PIECES):
+        pieces.append(rest.astype(jnp.bfloat16))
+        rest = rest - pieces[-1].astype(jnp.float32)
+    tail = jnp.concatenate(pieces + [acc[i].astype(jnp.bfloat16) for i in (1, 2)], axis=0)
     for j, shift in enumerate(list(order) + [0]):
         to = lax.rem(me + shift + n, n)
         u, q = to // quarter, lax.rem(to, quarter)
-        for k in range(kinds):
-            slots[j][k * part:(k + 1) * part, :] = x_ref[k, u, pl.ds(pl.multiple_of(q * part, part), part), :]
+
+        @pl.when(live_blocks(vb_ref[u], me, per_dev) > q * (part // BLOCK))
+        def _():
+            for k in range(kinds):
+                slots[j][k * part:(k + 1) * part, :] = x_ref[k, u, pl.ds(pl.multiple_of(q * part, part), part), :]
+
         slots[j][kinds * part:, :] = tail
 
 
@@ -89,9 +94,8 @@
     total = jnp.zeros((rows, head), jnp.float32)
     hi, lo = total - ceiling_value, total + ceiling_value
     for src in range(n):
-        a, b, top, bottom = (acc[src, i * rows:(i + 1) * rows, :] for i in range(4))
-        count = jnp.clip(blocks - src * (per_dev // BLOCK), 0, per_dev // BLOCK) * BLOCK
-        total = total + ((a + b) + count * ((top + bottom) * 0.5))
+        *pieces, top, bottom = (acc[src, i * rows:(i + 1) * rows, :] for i in range(PIECES + 2))
+        total = total + functools.reduce(jnp.add, pieces)
         hi = jnp.maximum(hi, top)
         lo = jnp.minimum(lo, bottom)
     c = total / (blocks * BLOCK)
@@ -99,7 +103,7 @@
     c_ref[...] = c
     s_ref[...] = s
     cs = [c_ref[pl.ds(k * users + u, 1), :] for k in range(kinds)]
-    ss = [s_ref[pl.ds(k * users + u, 1), :] for k in range(kinds)]
+    ss = [1.0 / s_ref[pl.ds(k * users + u, 1), :] for k in range(kinds)]
     blocks_here = vb_ref[u]
     for j in range(n):
         src = source[j]
@@ -111,7 +115,7 @@
             def _():
                 for k in range(kinds):
                     v = slots[j][k * part + b * BLOCK:k * part + (b + 1) * BLOCK, :].astype(jnp.float32)
-                    out_ref[k, pl.ds(at, BLOCK), :] = ((v - cs[k]) / ss[k]).astype(jnp.bfloat16)
+                    out_ref[k, pl.ds(at, BLOCK), :] = ((v - cs[k]) * ss[k]).astype(jnp.bfloat16)
 
             @pl.when(jnp.logical_not(live))
             def _():
@@ -133,7 +137,7 @@
     full = n * part
     order = shifts(n)
     x = kv_cache.reshape(kinds, users, per_dev, head)
-    tall = kinds * part + 4 * rows
+    tall = kinds * part + (PIECES + 2) * rows
     anys = pl.BlockSpec(memory_space=pl.ANY)
     vmem = pl.BlockSpec(memory_space=pltpu.VMEM)
     smem = pl.BlockSpec(memory_space=pltpu.SMEM)
@@ -161,7 +165,7 @@
         out_specs=[anys, vmem, vmem],
         scratch_shapes=[
             pltpu.VMEM((kinds, full, head), jnp.bfloat16),
-            pltpu.VMEM((n, 4 * rows, head), jnp.float32),
+            pltpu.VMEM((n, (PIECES + 2) * rows, head), jnp.float32),
             pltpu.SemaphoreType.DMA((kinds,)),
         ],
         compiler_params=pltpu.CompilerParams(vmem_limit_bytes=LIMIT),

time: 145 us -> 144 us (level)
  starting transfers between devices: 126 us -> 119 us
  waiting for transfers between devices: 12 us -> 16.2 us
    ppermute x15, starting transfers between devices: 126 us -> 119 us  [on_device(): lax.ppermute(slots[j], 'seq', [(s, (s + shift) % n) for s in range(n)])]
    ppermute x15, waiting for transfers between devices: 12 us -> 16.2 us  [on_device(): lax.ppermute(slots[j], 'seq', [(s, (s + shift) % n) for s in range(n)])]
  transfers between devices with their start and end apart: 15 -> 15, of which waited for: 7 -> 5; matrix products, arithmetic and copies ran while one was open for 0% -> 0% of each run, Pallas kernels for 0% -> 0%
where the time goes in v4:
time: 144 us; the launch traced here: 143 us
  starting transfers between devices  119 us (83%)
  waiting for transfers between devices  16.2 us (11%)
  Pallas kernels  6.11 us (4%)
    ppermute x15, starting transfers between devices, on_device(): lax.ppermute(slots[j], 'seq', [(s, (s + shift) % n) for s in range(n)])  119 us
    ppermute x15, waiting for transfers between devices, on_device(): lax.ppermute(slots[j], 'seq', [(s, (s + shift) % n) for s in range(n)])  16.2 us
    pallas_call x1, Pallas kernels, on_device(): pl.pallas_call(functools.partial(build_kernel, order), out_shape=[pltpu.V...  3.54 us
  transfers between devices with their start and end apart: 15, of which 5 were waited for; matrix products, arithmetic and copies ran while one was open for 0% of the time, Pallas kernels for 0%

profile of v4, /device:TPU:78, one launch (start us, length us, event | category | flops | bytes accessed | tf_op | source)
XLA Modules:
  0.0 142.6 jit_solution(15787056640893194896)
XLA Ops:
  0.6 3.5 %shard_map.49 = (bf16[544,128]{1,0:T(8,128)(2,1)S(1)}, bf16[544,128]{1,0:T(8,128)(2,1)S(1)}, bf16[544,128]{1,0:T(8,128)(2,1)S(1)}, bf16[544,128]{1,0:T(8,128)(2,...) custom-call(s32[4]{0:T(128)} %vb_ref.3, ...), custom_call_target="tpu_custom_call" | custom-call | tf_op jit(solution)/shard_map/pallas_call | solution.py:144
  4.2 32.2 %collective-permute-start = (bf16[544,128]{1,0:T(8,128)(2,1)S(1)}, bf16[544,128]{1,0:T(8,128)(2,1)S(1)}, u32[]{:S(2)}, u32[]{:S(2)}) collective-permute-start(bf16[544,128]{1,0:T(8,128)(2,1)S(1)} %get-tuple-element.22), channel_id=1, source_target_pairs={{0,128},{16,144},{32,160},{48,176},{64,192},{80,208},{96,224},{112... | collective-permute-start | bytes 417800 | tf_op jit(solution)/shard_map/ppermute | solution.py:157
  36.4 20.7 %collective-permute-start.1 = (bf16[544,128]{1,0:T(8,128)(2,1)S(1)}, bf16[544,128]{1,0:T(8,128)(2,1)S(1)}, u32[]{:S(2)}, u32[]{:S(2)}) collective-permute-start(bf16[544,128]{1,0:T(8,128)(2,1)S(1)} %get-tuple-element.23), channel_id=1, source_target_pairs={{0,112},{16,128},{32,144},{48,160},{64,176},{80,192},{96,208},{112... | collective-permute-start | bytes 417800 | tf_op jit(solution)/shard_map/ppermute | solution.py:157
  57.1 2.0 %collective-permute-start.2 = (bf16[544,128]{1,0:T(8,128)(2,1)S(1)}, bf16[544,128]{1,0:T(8,128)(2,1)S(1)}, u32[]{:S(2)}, u32[]{:S(2)}) collective-permute-start(bf16[544,128]{1,0:T(8,128)(2,1)S(1)} %get-tuple-element.24), channel_id=1, source_target_pairs={{0,144},{16,160},{32,176},{48,192},{64,208},{80,224},{96,240},{112... | collective-permute-start | bytes 417800 | tf_op jit(solution)/shard_map/ppermute | solution.py:157
  59.1 2.0 %collective-permute-start.3 = (bf16[544,128]{1,0:T(8,128)(2,1)S(1)}, bf16[544,128]{1,0:T(8,128)(2,1)S(1)}, u32[]{:S(2)}, u32[]{:S(2)}) collective-permute-start(bf16[544,128]{1,0:T(8,128)(2,1)S(1)} %get-tuple-element.25), channel_id=1, source_target_pairs={{0,160},{16,176},{32,192},{48,208},{64,224},{80,240},{96,0},{112,1... | collective-permute-start | bytes 417800 | tf_op jit(solution)/shard_map/ppermute | solution.py:157
  61.0 9.7 %collective-permute-start.4 = (bf16[544,128]{1,0:T(8,128)(2,1)S(1)}, bf16[544,128]{1,0:T(8,128)(2,1)S(1)}, u32[]{:S(2)}, u32[]{:S(2)}) collective-permute-start(bf16[544,128]{1,0:T(8,128)(2,1)S(1)} %get-tuple-element.26), channel_id=1, source_target_pairs={{0,96},{16,112},{32,128},{48,144},{64,160},{80,176},{96,192},{112,... | collective-permute-start | bytes 417800 | tf_op jit(solution)/shard_map/ppermute | solution.py:157
  70.7 0.0 collective-permute-done.refs_0_
  70.7 6.5 %collective-permute-start.5 = (bf16[544,128]{1,0:T(8,128)(2,1)S(1)}, bf16[544,128]{1,0:T(8,128)(2,1)S(1)}, u32[]{:S(2)}, u32[]{:S(2)}) collective-permute-start(bf16[544,128]{1,0:T(8,128)(2,1)S(1)} %get-tuple-element.27), channel_id=1, source_target_pairs={{0,80},{16,96},{32,112},{48,128},{64,144},{80,160},{96,176},{112,1... | collective-permute-start | bytes 417800 | tf_op jit(solution)/shard_map/ppermute | solution.py:157
  77.2 0.0 collective-permute-done.1.refs_1_
  77.3 5.4 %collective-permute-start.6 = (bf16[544,128]{1,0:T(8,128)(2,1)S(1)}, bf16[544,128]{1,0:T(8,128)(2,1)S(1)}, u32[]{:S(2)}, u32[]{:S(2)}) collective-permute-start(bf16[544,128]{1,0:T(8,128)(2,1)S(1)} %get-tuple-element.28), channel_id=1, source_target_pairs={{0,176},{16,192},{32,208},{48,224},{64,240},{80,0},{96,16},{112,32... | collective-permute-start | bytes 417800 | tf_op jit(solution)/shard_map/ppermute | solution.py:157
  82.7 2.4 %collective-permute-done.2.refs_2_ = bf16[544,128]{1,0:T(8,128)(2,1)S(1)} collective-permute-done((bf16[544,128]{1,0:T(8,128)(2,1)S(1)}, bf16[544,128]{1,0:T(8,128)(2,1)S(1)}, u32[]{:S(2)}, u32[]{:S(2)}) %collective-permute-start.2) | collective-permute-done | bytes 139296 | tf_op jit(solution)/shard_map/ppermute | solution.py:157
  85.1 7.9 %collective-permute-start.7 = (bf16[544,128]{1,0:T(8,128)(2,1)S(1)}, bf16[544,128]{1,0:T(8,128)(2,1)S(1)}, u32[]{:S(2)}, u32[]{:S(2)}) collective-permute-start(bf16[544,128]{1,0:T(8,128)(2,1)S(1)} %get-tuple-element.29), channel_id=1, source_target_pairs={{0,192},{16,208},{32,224},{48,240},{64,0},{80,16},{96,32},{112,48}... | collective-permute-start | bytes 417800 | tf_op jit(solution)/shard_map/ppermute | solution.py:157
  93.0 9.1 %collective-permute-done.3.refs_3_ = bf16[544,128]{1,0:T(8,128)(2,1)S(1)} collective-permute-done((bf16[544,128]{1,0:T(8,128)(2,1)S(1)}, bf16[544,128]{1,0:T(8,128)(2,1)S(1)}, u32[]{:S(2)}, u32[]{:S(2)}) %collective-permute-start.3) | collective-permute-done | bytes 139296 | tf_op jit(solution)/shard_map/ppermute | solution.py:157
  102.2 1.9 %collective-permute-start.8 = (bf16[544,128]{1,0:T(8,128)(2,1)S(1)}, bf16[544,128]{1,0:T(8,128)(2,1)S(1)}, u32[]{:S(2)}, u32[]{:S(2)}) collective-permute-start(bf16[544,128]{1,0:T(8,128)(2,1)S(1)} %get-tuple-element.30), channel_id=1, source_target_pairs={{0,64},{16,80},{32,96},{48,112},{64,128},{80,144},{96,160},{112,17... | collective-permute-start | bytes 417800 | tf_op jit(solution)/shard_map/ppermute | solution.py:157
  104.1 0.0 collective-permute-done.4.refs_4_
  104.1 15.2 %collective-permute-start.9 = (bf16[544,128]{1,0:T(8,128)(2,1)S(1)}, bf16[544,128]{1,0:T(8,128)(2,1)S(1)}, u32[]{:S(2)}, u32[]{:S(2)}) collective-permute-start(bf16[544,128]{1,0:T(8,128)(2,1)S(1)} %get-tuple-element.31), channel_id=1, source_target_pairs={{0,48},{16,64},{32,80},{48,96},{64,112},{80,128},{96,144},{112,160... | collective-permute-start | bytes 417800 | tf_op jit(solution)/shard_map/ppermute | solution.py:157
  119.3 0.0 collective-permute-done.5.refs_5_
  119.3 2.0 %collective-permute-start.10 = (bf16[544,128]{1,0:T(8,128)(2,1)S(1)}, bf16[544,128]{1,0:T(8,128)(2,1)S(1)}, u32[]{:S(2)}, u32[]{:S(2)}) collective-permute-start(bf16[544,128]{1,0:T(8,128)(2,1)S(1)} %get-tuple-element.32), channel_id=1, source_target_pairs={{0,208},{16,224},{32,240},{48,0},{64,16},{80,32},{96,48},{112,64},... | collective-permute-start | bytes 417800 | tf_op jit(solution)/shard_map/ppermute | solution.py:157
  121.3 0.0 collective-permute-done.6.refs_6_
  121.3 2.0 %collective-permute-start.11 = (bf16[544,128]{1,0:T(8,128)(2,1)S(1)}, bf16[544,128]{1,0:T(8,128)(2,1)S(1)}, u32[]{:S(2)}, u32[]{:S(2)}) collective-permute-start(bf16[544,128]{1,0:T(8,128)(2,1)S(1)} %get-tuple-element.33), channel_id=1, source_target_pairs={{0,224},{16,240},{32,0},{48,16},{64,32},{80,48},{96,64},{112,80},{... | collective-permute-start | bytes 417800 | tf_op jit(solution)/shard_map/ppermute | solution.py:157
  123.3 0.0 collective-permute-done.7.refs_7_
  123.3 5.0 %collective-permute-start.12 = (bf16[544,128]{1,0:T(8,128)(2,1)S(1)}, bf16[544,128]{1,0:T(8,128)(2,1)S(1)}, u32[]{:S(2)}, u32[]{:S(2)}) collective-permute-start(bf16[544,128]{1,0:T(8,128)(2,1)S(1)} %get-tuple-element.34), channel_id=1, source_target_pairs={{0,32},{16,48},{32,64},{48,80},{64,96},{80,112},{96,128},{112,144}... | collective-permute-start | bytes 417800 | tf_op jit(solution)/shard_map/ppermute | solution.py:157
  128.2 0.0 collective-permute-done.8.refs_8_
  128.3 3.3 %collective-permute-start.13 = (bf16[544,128]{1,0:T(8,128)(2,1)S(1)}, bf16[544,128]{1,0:T(8,128)(2,1)S(1)}, u32[]{:S(2)}, u32[]{:S(2)}) collective-permute-start(bf16[544,128]{1,0:T(8,128)(2,1)S(1)} %get-tuple-element.35), channel_id=1, source_target_pairs={{0,16},{16,32},{32,48},{48,64},{64,80},{80,96},{96,112},{112,128},... | collective-permute-start | bytes 417800 | tf_op jit(solution)/shard_map/ppermute | solution.py:157
  131.6 0.0 collective-permute-done.9.refs_9_
  131.6 3.8 %collective-permute-start.14 = (bf16[544,128]{1,0:T(8,128)(2,1)S(1)}, bf16[544,128]{1,0:T(8,128)(2,1)S(1)}, u32[]{:S(2)}, u32[]{:S(2)}) collective-permute-start(bf16[544,128]{1,0:T(8,128)(2,1)S(1)} %get-tuple-element.36), channel_id=1, source_target_pairs={{0,240},{16,0},{32,16},{48,32},{64,48},{80,64},{96,80},{112,96},{1... | collective-permute-start | bytes 417800 | tf_op jit(solution)/shard_map/ppermute | solution.py:157
  135.4 0.3 collective-permute-done.10.refs_10_
  135.7 4.1 %collective-permute-done.11.refs_11_ = bf16[544,128]{1,0:T(8,128)(2,1)S(1)} collective-permute-done((bf16[544,128]{1,0:T(8,128)(2,1)S(1)}, bf16[544,128]{1,0:T(8,128)(2,1)S(1)}, u32[]{:S(2)}, u32[]{:S(2)}) %collective-permute-start.11) | collective-permute-done | bytes 139296 | tf_op jit(solution)/shard_map/ppermute | solution.py:157
  139.8 0.0 collective-permute-done.12.refs_12_
  139.8 0.0 collective-permute-done.13.refs_13_
  139.8 0.3 collective-permute-done.14.refs_14_
  140.1 2.6 %shard_map.50 = (bf16[2,4096,128]{2,1,0:T(8,128)(2,1)}, f32[8,128]{1,0:T(8,128)}, f32[8,128]{1,0:T(8,128)}) custom-call(s32[4]{0:T(128)S(1)} %copy-done, bf16[544,128]{1,0:T(8,128)(2,1)S(1)} %collective-permute-done.refs_0_, bf16[544,128]{1,0:T(8,128)(2,1)S(1)} %collective-permute-done.1.refs_1_, bf16[544,128]{1,0:T(8,128)(2,1)S(1)} %collective-permute-done.2.refs_2_, ...), custom_call_target="tpu_custom_call" | custom-call | tf_op jit(solution)/shard_map/pallas_call | solution.py:161
  (2 shorter events, 0.0 us)
Async XLA Ops:
  0.6 139.4 %copy-start = (s32[4]{0:T(128)S(1)}, s32[4]{0:T(128)}, u32[]{:S(2)}) copy-start(s32[4]{0:T(128)} %vb_ref.3) | copy-start | bytes 52
  4.2 66.5 %collective-permute-start = (bf16[544,128]{1,0:T(8,128)(2,1)S(1)}, bf16[544,128]{1,0:T(8,128)(2,1)S(1)}, u32[]{:S(2)}, u32[]{:S(2)}) collective-permute-start(bf16[544,128]{1,0:T(8,128)(2,1)S(1)} %get-tuple-element.22), channel_id=1, source_target_pairs={{0,128},{16,144},{32,160},{48,176},{64,192},{80,208},{96,224},{112... | collective-permute-start | bytes 417800 | tf_op jit(solution)/shard_map/ppermute | solution.py:157
  36.4 40.9 %collective-permute-start.1 = (bf16[544,128]{1,0:T(8,128)(2,1)S(1)}, bf16[544,128]{1,0:T(8,128)(2,1)S(1)}, u32[]{:S(2)}, u32[]{:S(2)}) collective-permute-start(bf16[544,128]{1,0:T(8,128)(2,1)S(1)} %get-tuple-element.23), channel_id=1, source_target_pairs={{0,112},{16,128},{32,144},{48,160},{64,176},{80,192},{96,208},{112... | collective-permute-start | bytes 417800 | tf_op jit(solution)/shard_map/ppermute | solution.py:157
  57.1 27.9 %collective-permute-start.2 = (bf16[544,128]{1,0:T(8,128)(2,1)S(1)}, bf16[544,128]{1,0:T(8,128)(2,1)S(1)}, u32[]{:S(2)}, u32[]{:S(2)}) collective-permute-start(bf16[544,128]{1,0:T(8,128)(2,1)S(1)} %get-tuple-element.24), channel_id=1, source_target_pairs={{0,144},{16,160},{32,176},{48,192},{64,208},{80,224},{96,240},{112... | collective-permute-start | bytes 417800 | tf_op jit(solution)/shard_map/ppermute | solution.py:157
  59.1 43.1 %collective-permute-start.3 = (bf16[544,128]{1,0:T(8,128)(2,1)S(1)}, bf16[544,128]{1,0:T(8,128)(2,1)S(1)}, u32[]{:S(2)}, u32[]{:S(2)}) collective-permute-start(bf16[544,128]{1,0:T(8,128)(2,1)S(1)} %get-tuple-element.25), channel_id=1, source_target_pairs={{0,160},{16,176},{32,192},{48,208},{64,224},{80,240},{96,0},{112,1... | collective-permute-start | bytes 417800 | tf_op jit(solution)/shard_map/ppermute | solution.py:157
  61.0 43.1 %collective-permute-start.4 = (bf16[544,128]{1,0:T(8,128)(2,1)S(1)}, bf16[544,128]{1,0:T(8,128)(2,1)S(1)}, u32[]{:S(2)}, u32[]{:S(2)}) collective-permute-start(bf16[544,128]{1,0:T(8,128)(2,1)S(1)} %get-tuple-element.26), channel_id=1, source_target_pairs={{0,96},{16,112},{32,128},{48,144},{64,160},{80,176},{96,192},{112,... | collective-permute-start | bytes 417800 | tf_op jit(solution)/shard_map/ppermute | solution.py:157
  70.7 48.6 %collective-permute-start.5 = (bf16[544,128]{1,0:T(8,128)(2,1)S(1)}, bf16[544,128]{1,0:T(8,128)(2,1)S(1)}, u32[]{:S(2)}, u32[]{:S(2)}) collective-permute-start(bf16[544,128]{1,0:T(8,128)(2,1)S(1)} %get-tuple-element.27), channel_id=1, source_target_pairs={{0,80},{16,96},{32,112},{48,128},{64,144},{80,160},{96,176},{112,1... | collective-permute-start | bytes 417800 | tf_op jit(solution)/shard_map/ppermute | solution.py:157
  77.3 44.0 %collective-permute-start.6 = (bf16[544,128]{1,0:T(8,128)(2,1)S(1)}, bf16[544,128]{1,0:T(8,128)(2,1)S(1)}, u32[]{:S(2)}, u32[]{:S(2)}) collective-permute-start(bf16[544,128]{1,0:T(8,128)(2,1)S(1)} %get-tuple-element.28), channel_id=1, source_target_pairs={{0,176},{16,192},{32,208},{48,224},{64,240},{80,0},{96,16},{112,32... | collective-permute-start | bytes 417800 | tf_op jit(solution)/shard_map/ppermute | solution.py:157
  85.1 38.2 %collective-permute-start.7 = (bf16[544,128]{1,0:T(8,128)(2,1)S(1)}, bf16[544,128]{1,0:T(8,128)(2,1)S(1)}, u32[]{:S(2)}, u32[]{:S(2)}) collective-permute-start(bf16[544,128]{1,0:T(8,128)(2,1)S(1)} %get-tuple-element.29), channel_id=1, source_target_pairs={{0,192},{16,208},{32,224},{48,240},{64,0},{80,16},{96,32},{112,48}... | collective-permute-start | bytes 417800 | tf_op jit(solution)/shard_map/ppermute | solution.py:157
  102.2 26.1 %collective-permute-start.8 = (bf16[544,128]{1,0:T(8,128)(2,1)S(1)}, bf16[544,128]{1,0:T(8,128)(2,1)S(1)}, u32[]{:S(2)}, u32[]{:S(2)}) collective-permute-start(bf16[544,128]{1,0:T(8,128)(2,1)S(1)} %get-tuple-element.30), channel_id=1, source_target_pairs={{0,64},{16,80},{32,96},{48,112},{64,128},{80,144},{96,160},{112,17... | collective-permute-start | bytes 417800 | tf_op jit(solution)/shard_map/ppermute | solution.py:157
  104.1 27.5 %collective-permute-start.9 = (bf16[544,128]{1,0:T(8,128)(2,1)S(1)}, bf16[544,128]{1,0:T(8,128)(2,1)S(1)}, u32[]{:S(2)}, u32[]{:S(2)}) collective-permute-start(bf16[544,128]{1,0:T(8,128)(2,1)S(1)} %get-tuple-element.31), channel_id=1, source_target_pairs={{0,48},{16,64},{32,80},{48,96},{64,112},{80,128},{96,144},{112,160... | collective-permute-start | bytes 417800 | tf_op jit(solution)/shard_map/ppermute | solution.py:157
  119.3 16.3 %collective-permute-start.10 = (bf16[544,128]{1,0:T(8,128)(2,1)S(1)}, bf16[544,128]{1,0:T(8,128)(2,1)S(1)}, u32[]{:S(2)}, u32[]{:S(2)}) collective-permute-start(bf16[544,128]{1,0:T(8,128)(2,1)S(1)} %get-tuple-element.32), channel_id=1, source_target_pairs={{0,208},{16,224},{32,240},{48,0},{64,16},{80,32},{96,48},{112,64},... | collective-permute-start | bytes 417800 | tf_op jit(solution)/shard_map/ppermute | solution.py:157
  121.3 18.5 %collective-permute-start.11 = (bf16[544,128]{1,0:T(8,128)(2,1)S(1)}, bf16[544,128]{1,0:T(8,128)(2,1)S(1)}, u32[]{:S(2)}, u32[]{:S(2)}) collective-permute-start(bf16[544,128]{1,0:T(8,128)(2,1)S(1)} %get-tuple-element.33), channel_id=1, source_target_pairs={{0,224},{16,240},{32,0},{48,16},{64,32},{80,48},{96,64},{112,80},{... | collective-permute-start | bytes 417800 | tf_op jit(solution)/shard_map/ppermute | solution.py:157
  123.3 16.5 %collective-permute-start.12 = (bf16[544,128]{1,0:T(8,128)(2,1)S(1)}, bf16[544,128]{1,0:T(8,128)(2,1)S(1)}, u32[]{:S(2)}, u32[]{:S(2)}) collective-permute-start(bf16[544,128]{1,0:T(8,128)(2,1)S(1)} %get-tuple-element.34), channel_id=1, source_target_pairs={{0,32},{16,48},{32,64},{48,80},{64,96},{80,112},{96,128},{112,144}... | collective-permute-start | bytes 417800 | tf_op jit(solution)/shard_map/ppermute | solution.py:157
  128.3 11.5 %collective-permute-start.13 = (bf16[544,128]{1,0:T(8,128)(2,1)S(1)}, bf16[544,128]{1,0:T(8,128)(2,1)S(1)}, u32[]{:S(2)}, u32[]{:S(2)}) collective-permute-start(bf16[544,128]{1,0:T(8,128)(2,1)S(1)} %get-tuple-element.35), channel_id=1, source_target_pairs={{0,16},{16,32},{32,48},{48,64},{64,80},{80,96},{96,112},{112,128},... | collective-permute-start | bytes 417800 | tf_op jit(solution)/shard_map/ppermute | solution.py:157
  131.6 8.5 %collective-permute-start.14 = (bf16[544,128]{1,0:T(8,128)(2,1)S(1)}, bf16[544,128]{1,0:T(8,128)(2,1)S(1)}, u32[]{:S(2)}, u32[]{:S(2)}) collective-permute-start(bf16[544,128]{1,0:T(8,128)(2,1)S(1)} %get-tuple-element.36), channel_id=1, source_target_pairs={{0,240},{16,0},{32,16},{48,32},{64,48},{80,64},{96,80},{112,96},{1... | collective-permute-start | bytes 417800 | tf_op jit(solution)/shard_map/ppermute | solution.py:157
